TPU v7x, 32 devices: a whole 2x2x4 slice. The times are simulated.
32 devices in a mesh: chan: 16 (over z, y, core), tm: 2 (over x).
Axes of the slice: x: 2, y: 2, z: 4, core: 2. Of those that a mesh axis runs over, the one named last changes fastest.
Arguments:
- voltages: bfloat16 [2, 512, 256, 512], P(None, None, 'chan', 'tm'), may hold values from -6 to 6, as said below
- flag_mask: int32 [4, 256], P('tm', 'chan'), may hold values from 0 to 1, as said below
- flagged_prefix_counts: int32 [4, 256], P('tm', 'chan'), may hold values from 0 to 127
Outputs:
- visibilities: float32 [512, 2, 256, 256], P(('chan', 'tm'))
Inputs may be any that keep to these rules, and one draw needn't show every extreme that they name: `voltages`: samples that keep drops count as zero; a program may move only the kept samples, in any compact form. `flag_mask`: 1 keeps the block of 128 samples of an antenna, 0 drops it; some antennas are dropped in every block. The first flagged_prefix_counts samples of a kept block are flagged; flags and counts may be packed several to a word wherever they are moved.
All inputs are finite; a program needn't handle non-finite values.
Results may differ from a plain program's by a relative error of at most 0.0003.
Values may be sent and summed in bfloat16 or wider, within the bound.
A program may use at most 128 MiB of HBM per device.

v0:
```python
import jax
import jax.numpy as jnp
from jax import lax
from jax.sharding import PartitionSpec as P

FLAG_BLOCK_WIDTH = 128


def pair_samples(flag_mask, flagged_prefix_counts):

    def add_block(total, block):
        live = block[0].astype(jnp.float32)
        cover = (FLAG_BLOCK_WIDTH - jnp.maximum(block[1][:, None], block[1][None, :])).astype(
            jnp.float32
        )
        return (total + live[:, None] * live[None, :] * cover, 0)

    start = jnp.zeros((flag_mask.shape[1], flag_mask.shape[1]), jnp.float32)
    total, unused = lax.scan(add_block, start, (flag_mask, flagged_prefix_counts))
    return total


def cross_products(slab):
    real_part, imag_part = (slab[0], slab[1])
    rr = jnp.einsum("cit,cjt->cij", real_part, real_part, preferred_element_type=jnp.float32)
    ii = jnp.einsum("cit,cjt->cij", imag_part, imag_part, preferred_element_type=jnp.float32)
    ir = jnp.einsum("cit,cjt->cij", imag_part, real_part, preferred_element_type=jnp.float32)
    ri = jnp.einsum("cit,cjt->cij", real_part, imag_part, preferred_element_type=jnp.float32)
    real_out = rr + ii
    imag_out = ir - ri
    return jnp.stack([real_out, imag_out], axis=1)


def shards(voltages, flag_mask, flagged_prefix_counts):
    antenna_slice = voltages.shape[2]
    sample_slice = voltages.shape[3]
    offsets = jnp.arange(FLAG_BLOCK_WIDTH, dtype=jnp.int32)
    retain_mask = (flag_mask.T[:, :, None] == 1) & (
        offsets[None, None, :] >= flagged_prefix_counts.T[:, :, None]
    )
    retain_mask = retain_mask.reshape(antenna_slice, sample_slice)
    masked = jnp.where(retain_mask[None, None], voltages, jnp.zeros((), voltages.dtype))
    all_mask, all_counts = (
        lax.all_gather(flag_mask, "chan", axis=1, tiled=True),
        lax.all_gather(flagged_prefix_counts, "chan", axis=1, tiled=True),
    )
    all_mask, all_counts = (
        lax.all_gather(all_mask, "tm", axis=0, tiled=True),
        lax.all_gather(all_counts, "tm", axis=0, tiled=True),
    )
    pairs = pair_samples(all_mask, all_counts)
    turned = lax.all_to_all(masked, "chan", split_axis=1, concat_axis=2, tiled=True)
    summed = lax.psum_scatter(cross_products(turned), "tm", scatter_dimension=0, tiled=True)
    return summed / jnp.maximum(pairs, 1.0)[None, None]


def solution(mesh):
    placed = (P(None, None, "chan", "tm"), P("tm", "chan"), P("tm", "chan"))
    return jax.shard_map(
        shards,
        mesh=mesh,
        in_specs=placed,
        out_specs=P(("chan", "tm"), None, None, None),
        check_vma=False,
    )
```

profile of v0, /device:TPU:0, one launch (start us, length us, event | category | flops | bytes accessed | tf_op | source)
XLA Modules:
  0.0 464.3 jit_solution(6342029855375286497)
XLA Ops:
  6.5 0.8 copy.15
  7.3 0.7 compare_bitcast_fusion
  8.3 7.3 %copy_select_fusion = bf16[2,512,16,256]{3,2,0,1:T(8,128)(2,1)} fusion(bf16[2,512,16,256]{3,2,1,0:T(8,128)(2,1)} %param.5, pred[16,256]{1,0:T(8,128)(4,1)S(1)} %fusion), kind=kLoop, calls=%fused_computation.6 | loop fusion | flops 4194304 | bytes 16781312 | tf_op jit(solution)/shard_map/jit(_where)/select_n | solution.py:42
  15.6 189.5 %all_to_all.15 = bf16[2,512,16,256]{3,2,0,1:T(8,128)(2,1)} all-to-all(bf16[2,512,16,256]{3,2,0,1:T(8,128)(2,1)} %copy_select_fusion), channel_id=1, replica_groups=mesh['chan'=16,'tm'=2] {'chan'}, dimensions={1} | all-to-all | bytes 16777216 | tf_op jit(solution)/shard_map/all_to_all | solution.py:52
  205.1 8.0 %copy.34 = bf16[2,16,32,16,256]{4,3,1,2,0:T(8,128)(2,1)} copy(bf16[2,16,32,16,256]{4,3,0,2,1:T(8,128)(2,1)} %bitcast.71) | data formatting | bytes 16777216 | tf_op jit(solution)/shard_map/all_to_all | solution.py:52
  213.1 3.8 fusion.1
  216.9 1.3 fusion.2
  218.2 4.7 %fusion.3 = f32[32,256,256]{2,1,0:T(8,128)} fusion(bf16[32,256,256]{2,1,0:T(8,128)(2,1)S(1)} %bitcast.61, bf16[32,256,256]{2,1,0:T(8,128)(2,1)S(1)} %bitcast.65), kind=kOutput, calls=%fused_computation.16 | convolution fusion | flops 1073741824 | bytes 16777216 | tf_op jit(solution)/shard_map/cit,cjt->cij/dot_general | solution.py:27
  222.9 8.2 %subtract_bitcast_fusion = f32[32,1,256,256]{3,2,0,1:T(8,128)} fusion(f32[32,256,256]{2,1,0:T(8,128)} %fusion.3, bf16[32,256,256]{2,1,0:T(8,128)(2,1)S(1)} %bitcast.66, bf16[32,256,256]{2,1,0:T(8,128)(2,1)S(1)} %bitcast.62), kind=kOutput, calls=%fused_computation.7 | convolution fusion | flops 1075838976 | bytes 25165824 | tf_op jit(solution)/shard_map/cit,cjt->cij/dot_general | solution.py:28
  231.1 4.5 add_bitcast_fusion
  235.7 6.9 %pad_maximum_fusion = f32[32,2,256,256]{3,2,0,1:T(8,128)S(1)} fusion(f32[32,1,256,256]{3,2,0,1:T(8,128)} %subtract_bitcast_fusion, f32[32,1,256,256]{3,2,0,1:T(8,128)} %add_bitcast_fusion), kind=kLoop, calls=%fused_computation.3 | loop fusion | flops 4194304 | bytes 33554432 | tf_op jit(solution)/shard_map/stack | solution.py:31
  242.6 1.6 copy.21
  244.2 11.7 %copy.25 = f32[4,8,512,256]{3,1,2,0:T(8,128)} copy(f32[4,8,512,256]{3,2,1,0:T(8,128)S(1)} %bitcast.68) | data formatting | bytes 33554432
  255.9 0.6 copy-done.1
  256.6 21.4 %all-gather = s32[16,16,2]{1,2,0:T(2,128)S(1)} all-gather(s32[1,16,2]{1,2,0:T(2,128)S(1)} %bitcast.81), channel_id=1, replica_groups=mesh['chan'=16,'tm'=2] {'chan'}, dimensions={0}, use_global_device_ids=true | all-gather | bytes 2176 | tf_op jit(solution)/shard_map/all_gather | solution.py:44
  278.1 4.5 all-gather.1
  282.6 17.2 %all-gather.2 = s32[16,16,2]{1,2,0:T(2,128)S(1)} all-gather(s32[1,16,2]{1,2,0:T(2,128)S(1)} %bitcast.80), channel_id=1, replica_groups=mesh['chan'=16,'tm'=2] {'chan'}, dimensions={0}, use_global_device_ids=true | all-gather | bytes 2176 | tf_op jit(solution)/shard_map/all_gather | solution.py:45
  299.9 4.7 %all-gather.3 = s32[2,2,256]{2,1,0:T(2,128)S(1)} all-gather(s32[1,2,256]{2,1,0:T(2,128)S(1)} %bitcast.78), channel_id=1, replica_groups=mesh['chan'=16,'tm'=2] {'tm'}, dimensions={0}, use_global_device_ids=true | all-gather | bytes 6144 | tf_op jit(solution)/shard_map/all_gather | solution.py:49
  304.6 0.8 while.11
  304.6 0.2 select_add_fusion.2
  305.4 141.0 %reduce-scatter.5.cloned.1.call-done = f32[16,131072]{1,0:T(8,128)} async-done(((f32[32,131072]{1,0:T(8,128)}), f32[16,131072]{1,0:T(8,128)}) %reduce-scatter.5.cloned.1.call-update) | async-done | bytes 8388624
  446.4 5.9 %copy.26 = f32[2,8,512,256]{3,2,1,0:T(8,128)S(1)} copy(f32[2,8,512,256]{3,1,2,0:T(8,128)} %bitcast.72) | data formatting | bytes 16777216
  452.3 1.1 copy_divide_fusion
  453.4 4.0 copy.20
  (25 shorter events, 1.0 us)
Async XLA Ops:
  6.5 439.9 %reduce-scatter.5.cloned.1.call-start = ((), (), s32[]{:S(2)}) async-start(), calls=%async_computation.2 | async-start | bytes 25165824
  255.9 0.7 copy-start.1
  255.9 26.7 %copy-start = (s32[2,16]{1,0:T(2,128)S(1)}, s32[2,16]{1,0:T(2,128)}, u32[]{:S(2)}) copy-start(s32[2,16]{1,0:T(2,128)} %param.7) | copy-start | bytes 388
Sparse Core Ops, SparseCore 0:
  256.0 190.3 reduce-scatter.4
where the time goes:
time: 465 us; the launch traced here: 464 us
  blocking collectives  237 us (51%)
  waiting for transfers between devices  141 us (30%)
  local copies, waits for them, and re-layouts  36.9 us (8%)
  matrix products  18.7 us (4%)
  other arithmetic  16.7 us (4%)
  between operations  13.5 us (3%)
    all_to_all x1, blocking collectives, shards(): lax.all_to_all(masked, 'chan', split_axis=1, concat_axis=2, tiled=True)  189 us
    unnamed x2, waiting for transfers between devices  141 us
    all_gather x1, blocking collectives, shards(): lax.all_gather(flag_mask, 'chan', axis=1, tiled=True)  21.4 us
    unnamed x11, local copies, waits for them, and re-layouts  20 us
    all_gather x1, blocking collectives, shards(): lax.all_gather(flagged_prefix_counts, 'chan', axis=1, tiled=True)  17.2 us
  transfers between devices with their start and end apart: 1, of which 1 were waited for; matrix products, arithmetic and copies ran while one was open for 0% of the time, Pallas kernels for 0%

commit v1 on v0

v1 whole, which is shorter than its diff:
```python
import functools

import jax
import jax.numpy as jnp
from jax import lax
from jax.experimental import pallas as pl
from jax.experimental.pallas import tpu as pltpu
from jax.sharding import PartitionSpec as P

FLAG_BLOCK_WIDTH = 128
LANES = 128
MESH = pl.DeviceIdType.MESH
NT = (((1,), (1,)), ((), ()))


def exchange_kernel(
    n_chan, n_tm, spans, volt_ref, mask_ref, count_ref, out_ref,
    held, masks, counts, square, cols, keep, inverse, send_sem, recv_sem, table_send, table_recv,
):
    n = n_chan * n_tm
    channels = held.shape[1]
    groups = range(len(spans))
    antennas, samples = volt_ref.shape[2], volt_ref.shape[3]
    total_antennas = n_chan * antennas
    local_blocks = samples // FLAG_BLOCK_WIDTH
    my_chan, my_tm = lax.axis_index("chan"), lax.axis_index("tm")
    me = my_chan * n_tm + my_tm

    def swing(m):
        return (m + 1) // 2 * (1 - 2 * lax.rem(m + 1, 2))

    def hop(k):
        return n // 2 + swing(k - 1)

    def place(k):
        other = lax.rem(me + hop(k), n)
        return other, (other // n_tm, lax.rem(other, n_tm))

    barrier = pltpu.get_barrier_semaphore()

    def greet(k, carry):
        pl.semaphore_signal(barrier, inc=1, device_id=place(k)[1], device_id_type=MESH)
        return carry

    lax.fori_loop(1, n, greet, 0)
    pl.semaphore_wait(barrier, n - 1)

    def landing(g):
        return held.at[
            :, pl.ds(*spans[g]), my_chan, :, pl.ds(pl.multiple_of(my_tm * samples, LANES), samples)
        ]

    def flag_copy(k, which):
        source, table = ((mask_ref, masks), (count_ref, counts))[which]
        return pltpu.make_async_remote_copy(
            src_ref=source, dst_ref=table.at[me], send_sem=table_send.at[which, k],
            recv_sem=table_recv.at[which], device_id=place(k)[1], device_id_type=MESH,
        )

    def volt_copy(g, k):
        other, where = place(k)
        return pltpu.make_async_remote_copy(
            src_ref=volt_ref.at[:, pl.ds(other * channels + spans[g][0], spans[g][1])],
            dst_ref=landing(g), send_sem=send_sem.at[g, k], recv_sem=recv_sem.at[g],
            device_id=where, device_id_type=MESH,
        )

    def each(body):
        def run(k, carry):
            body(k)
            return carry

        lax.fori_loop(1, n, run, 0)

    for which in range(2):
        each(lambda k, which=which: flag_copy(k, which).start())
    for g in groups:
        each(lambda k, g=g: volt_copy(g, k).start())
    pltpu.make_async_copy(mask_ref, masks.at[me], table_recv.at[0]).start()
    pltpu.make_async_copy(count_ref, counts.at[me], table_recv.at[1]).start()
    for g in groups:
        pltpu.make_async_copy(
            volt_ref.at[:, pl.ds(me * channels + spans[g][0], spans[g][1])], landing(g), recv_sem.at[g]
        ).start()

    pltpu.make_async_copy(masks, masks, table_recv.at[0]).wait()
    pltpu.make_async_copy(counts, counts, table_recv.at[1]).wait()
    limits = jnp.where(masks[...] == 1, counts[...], FLAG_BLOCK_WIDTH).astype(jnp.float32)
    square[...] = jnp.zeros_like(square)
    for b in range(local_blocks):
        square[b, :n, :antennas] = limits[:, b, :]
    turned = [square[b].T for b in range(local_blocks)]
    lane = lax.broadcasted_iota(jnp.int32, (total_antennas, LANES), 1).astype(jnp.float32)
    pairs = jnp.zeros((total_antennas, total_antennas), jnp.float32)
    for t in range(n_tm):
        for b in range(local_blocks):
            q = t * local_blocks + b
            for c in range(n_chan):
                source = c * n_tm + t
                cols[c * antennas:(c + 1) * antennas, :] = jnp.broadcast_to(
                    turned[b][:antennas, source:source + 1], (antennas, LANES)
                )
            column = cols[...]
            keep[:, q * LANES:(q + 1) * LANES] = jnp.where(lane >= column, 1.0, 0.0).astype(keep.dtype)
            pairs += FLAG_BLOCK_WIDTH - jnp.maximum(column[:, :1], column.T[:1, :])
    inverse[...] = 1.0 / jnp.maximum(pairs, 1.0)

    def correlate(c, carry):
        size = (total_antennas, keep.shape[1])
        real = held[0, c].reshape(size) * keep[...]
        imag = held[1, c].reshape(size) * keep[...]
        same = lax.dot_general(real, real, NT, preferred_element_type=jnp.float32)
        same += lax.dot_general(imag, imag, NT, preferred_element_type=jnp.float32)
        cross = lax.dot_general(imag, real, NT, preferred_element_type=jnp.float32)
        out_ref[c, 0] = same * inverse[...]
        out_ref[c, 1] = (cross - cross.T) * inverse[...]
        return carry

    for g in groups:
        part = held.at[:, pl.ds(*spans[g])]
        pltpu.make_async_copy(part, part, recv_sem.at[g]).wait()
        lax.fori_loop(spans[g][0], sum(spans[g]), correlate, 0)

    for which in range(2):
        each(lambda k, which=which: flag_copy(k, which).wait_send())
    for g in groups:
        each(lambda k, g=g: volt_copy(g, k).wait_send())


def shards(n_chan, n_tm, voltages, flag_mask, flagged_prefix_counts):
    parts, all_channels, antennas, samples = voltages.shape
    n = n_chan * n_tm
    channels = all_channels // n
    total_antennas, total_samples = antennas * n_chan, samples * n_tm
    last = max(1, channels // 8)
    cuts = [(channels - last) * g // 3 for g in range(4)] + [channels]
    spans = [(a, b - a) for a, b in zip(cuts, cuts[1:]) if b > a]
    groups, blocks = len(spans), flag_mask.shape[0]
    return pl.pallas_call(
        functools.partial(exchange_kernel, n_chan, n_tm, spans),
        out_shape=pltpu.VMEM((channels, 2, total_antennas, total_antennas), jnp.float32),
        in_specs=[pl.BlockSpec(memory_space=pl.ANY)] * 3,
        out_specs=pl.BlockSpec(memory_space=pltpu.VMEM),
        scratch_shapes=[
            pltpu.VMEM((parts, channels, n_chan, antennas, total_samples), voltages.dtype),
            pltpu.VMEM((n, blocks, antennas), jnp.int32),
            pltpu.VMEM((n, blocks, antennas), jnp.int32),
            pltpu.VMEM((blocks, n + -n % LANES, LANES), jnp.float32),
            pltpu.VMEM((total_antennas, LANES), jnp.float32),
            pltpu.VMEM((total_antennas, total_samples), voltages.dtype),
            pltpu.VMEM((total_antennas, total_antennas), jnp.float32),
            pltpu.SemaphoreType.DMA((groups, n)),
            pltpu.SemaphoreType.DMA((groups,)),
            pltpu.SemaphoreType.DMA((2, n)),
            pltpu.SemaphoreType.DMA((2,)),
        ],
        compiler_params=pltpu.CompilerParams(
            collective_id=0, has_side_effects=True, vmem_limit_bytes=48 * 1024 * 1024
        ),
    )(voltages, flag_mask, flagged_prefix_counts)


def solution(mesh):
    placed = (P(None, None, "chan", "tm"), P("tm", "chan"), P("tm", "chan"))
    return jax.shard_map(
        functools.partial(shards, mesh.shape["chan"], mesh.shape["tm"]),
        mesh=mesh,
        in_specs=placed,
        out_specs=P(("chan", "tm"), None, None, None),
        check_vma=False,
    )
```

time: 465 us -> 198 us (0.43)
  blocking collectives: 237 us -> 0 us
  Pallas kernels: 0 us -> 195 us
  waiting for transfers between devices: 141 us -> 0 us
  local copies, waits for them, and re-layouts: 36.9 us -> 3.4 us
  matrix products: 18.7 us -> 0 us
  other arithmetic: 16.7 us -> 0 us
  between operations: 13.5 us -> 0.01 us
    pallas_call x0 -> x1, Pallas kernels: none -> 195 us  [shards(): pl.pallas_call(functools.partial(exchange_kernel, n_chan, n_tm, spans), o...]
    all_to_all x1 -> x0, blocking collectives: 189 us -> none  [shards(): lax.all_to_all(masked, 'chan', split_axis=1, concat_axis=2, tiled=True)]
    unnamed x2 -> x0, waiting for transfers between devices: 141 us -> none
    all_gather x4 -> x0, blocking collectives: 47.8 us -> none  [the longest x1 21.4 us: shards(): lax.all_gather(flag_mask, 'chan', axis=1, tiled=True)]
    dot_general x4 -> x0, matrix products: 18.7 us -> none  [the longest x1 8.22 us: cross_products(): jnp.einsum('cit,cjt->cij', real_part, imag_part, preferred_element_type=j...]
    unnamed x11 -> x1, local copies, waits for them, and re-layouts: 20 us -> 3.4 us
    all_to_all x1 -> x0, local copies, waits for them, and re-layouts: 8.01 us -> none  [shards(): lax.all_to_all(masked, 'chan', split_axis=1, concat_axis=2, tiled=True)]
    select_n x1 -> x0, other arithmetic: 7.32 us -> none  [shards(): jnp.where(retain_mask[None, None], voltages, jnp.zeros((), voltages.dtype))]
  transfers between devices with their start and end apart: 1 -> 0, of which waited for: 1 -> 0; matrix products, arithmetic and copies ran while one was open for 0% -> 0% of each run, Pallas kernels for 0% -> 0%
where the time goes in v1:
time: 198 us
  Pallas kernels  195 us (98%)
  local copies, waits for them, and re-layouts  3.4 us (2%)
    pallas_call x1, Pallas kernels, shards(): pl.pallas_call(functools.partial(exchange_kernel, n_chan, n_tm, spans), o...  195 us

profile of v1, /device:TPU:0, one launch (start us, length us, event | category | flops | bytes accessed | tf_op | source)
XLA Modules:
  0.0 198.0 jit_solution(8408273229544434202)
XLA Ops:
  0.0 194.6 %shard_map.37 = f32[16,2,256,256]{3,2,1,0:T(8,128)S(1)} custom-call(bf16[2,512,16,256]{3,2,1,0:T(8,128)(2,1)} %volt_ref.1, s32[2,16]{1,0:T(2,128)} %mask_ref.1, s32[2,16]{1,0:T(2,128)} %count_ref.1), custom_call_target="tpu_custom_call" | custom-call | tf_op jit(solution)/shard_map/pallas_call | solution.py:139
  194.6 3.4 %copy.5 = f32[16,2,256,256]{3,2,1,0:T(8,128)} copy(f32[16,2,256,256]{3,2,1,0:T(8,128)S(1)} %shard_map.37) | data formatting | bytes 16777216
